TPU v7x, 32 devices: a whole 2x2x4 slice. The times are simulated.
32 devices in a mesh: rowa: 2 (over x), rowb: 4 (over z), col: 4 (over y, core).
Axes of the slice: x: 2, y: 2, z: 4, core: 2. Of those that a mesh axis runs over, the one named last changes fastest.
Arguments:
- table: float32 [65536, 512], P(('rowa', 'rowb'), 'col'), may hold values from -12 to 12
- start: float32 [16, 512], P(None, 'col'), may hold values from -6 to 6
Outputs:
- right_vectors: float32 [16, 512], P(None, 'col')
- left_images: float32 [16, 65536], P(None, ('rowa', 'rowb'))
- strengths: float32 [16], replicated
All inputs are finite; a program needn't handle non-finite values.
Results may differ from a plain program's by a relative error of at most 0.00014.
Values sent between devices are 32-bit elements.
A program may use at most 64 MiB of HBM per device.

v0:
```python
import jax
import jax.numpy as jnp
from jax import lax
from jax.sharding import PartitionSpec as P

STEPS = 8


high = lax.Precision.HIGHEST


def apply_rows(vectors, table):
    return lax.dot_general(
        vectors, table, (((1,), (1,)), ((), ())), precision=high, preferred_element_type=jnp.float32
    )


def outer_gram(products):
    return lax.dot_general(
        products,
        products,
        (((1,), (1,)), ((), ())),
        precision=high,
        preferred_element_type=jnp.float32,
    )


def normalize(gram, products):
    lower = jnp.linalg.cholesky(gram)
    return (jax.scipy.linalg.solve_triangular(lower, products, lower=True), lower)


def own_columns(vectors, start):
    width = start.shape[1]
    offset = lax.axis_index("col") * width
    return lax.dynamic_slice_in_dim(vectors, offset, width, 1)


def on_device(table, start):
    regrouped = lax.all_to_all(table, "col", split_axis=0, concat_axis=1, tiled=True)
    rows_total = table.shape[0] * lax.axis_size("rowa") * lax.axis_size("rowb")
    vectors = lax.all_gather(start, "col", axis=1, tiled=True)
    partial_cover = lax.dot_general(
        regrouped,
        regrouped,
        (((0,), (0,)), ((), ())),
        precision=high,
        preferred_element_type=jnp.float32,
    )
    cover = lax.psum(partial_cover, ("rowa", "rowb", "col"))
    previous = vectors
    lower = None
    for step in range(STEPS):
        previous = vectors
        products = jnp.dot(vectors, cover, precision=high, preferred_element_type=jnp.float32)
        vectors, lower = normalize(outer_gram(products), products)
    images = apply_rows(previous, regrouped)
    left = lax.all_gather(images, "col", axis=1, tiled=True)
    return (own_columns(vectors, start), left, jnp.diagonal(lower) / rows_total)


def solution(mesh):
    placed = (P(("rowa", "rowb"), "col"), P(None, "col"))
    return jax.shard_map(
        on_device,
        mesh=mesh,
        in_specs=placed,
        out_specs=(P(None, "col"), P(None, ("rowa", "rowb")), P()),
        check_vma=False,
    )
```

profile of v0, /device:TPU:0, one launch (start us, length us, event | category | flops | bytes accessed | tf_op | source)
XLA Modules:
  0.0 275.0 jit_solution(15089997109972043354)
XLA Ops:
  7.2 54.6 %all_to_all.19 = f32[4,2048,128]{2,1,0:T(8,128)} all-to-all(f32[4,2048,128]{2,1,0:T(8,128)} %bitcast.126), channel_id=1, replica_groups=mesh['rowa'=2,'rowb'=4,'col'=4] {'col'}, dimensions={0} | all-to-all | bytes 8388608 | tf_op jit(solution)/shard_map/all_to_all | solution.py:40
  61.8 5.4 %copy.21 = f32[2048,4,128]{0,2,1:T(8,128)} copy(f32[2048,4,128]{2,0,1:T(8,128)} %bitcast.125) | data formatting | bytes 8388608 | tf_op jit(solution)/shard_map/all_to_all | solution.py:40
  67.1 10.3 %fusion.48 = f32[512,512]{1,0:T(8,128)} fusion(f32[2048,512]{0,1:T(8,128)} %bitcast.123), kind=kOutput, calls=%fused_computation.78 | convolution fusion | flops 6442450944 | bytes 5242880 | tf_op jit(solution)/shard_map/dot_general | solution.py:43
  77.5 5.4 %all_gather.6 = f32[16,512]{1,0:T(8,128)S(1)} all-gather(f32[16,128]{1,0:T(8,128)S(1)} %copy-done.1), channel_id=1, replica_groups=mesh['rowa'=2,'rowb'=4,'col'=4] {'col'}, dimensions={1}, use_global_device_ids=true | all-gather | bytes 40960 | tf_op jit(solution)/shard_map/all_gather | solution.py:42
  82.9 126.5 %all-reduce.2.cloned.1.call-done = f32[512,512]{1,0:T(8,128)} async-done(((f32[512,512]{1,0:T(8,128)}), f32[512,512]{1,0:T(8,128)}) %all-reduce.2.cloned.1.call-update) | async-done | bytes 1048592 | tf_op jit(solution)/shard_map/psum | solution.py:50
  209.4 2.0 fusion.49
  211.6 1.5 cholesky.134
  213.7 0.6 fusion.2
  214.4 1.2 custom-call.14
  215.8 1.9 fusion.51
  217.9 1.5 cholesky.145
  220.1 0.6 fusion.3
  220.7 1.2 custom-call.15
  222.2 1.9 fusion.53
  224.3 1.5 cholesky.156
  226.4 0.6 fusion.4
  227.1 1.2 custom-call.16
  229.4 1.5 cholesky.167
  231.6 0.6 fusion.5
  232.2 1.2 custom-call.17
  234.6 1.5 cholesky.178
  237.4 1.2 custom-call.18
  239.7 1.5 cholesky.189
  242.5 1.2 custom-call.19
  244.8 1.5 cholesky.200
  247.6 1.2 custom-call.20
  249.1 4.3 %fusion.65 = f32[16,2048]{1,0:T(8,128)S(1)} fusion(f32[16,512]{1,0:T(8,128)S(1)} %fusion.12, f32[2048,512]{0,1:T(8,128)} %bitcast.124), kind=kOutput, calls=%fused_computation.95 | convolution fusion | flops 201326592 | bytes 4358144 | tf_op jit(solution)/shard_map/dot_general | solution.py:13
  253.4 7.1 %all_gather.7 = f32[16,8192]{1,0:T(8,128)S(1)} all-gather(f32[16,2048]{1,0:T(8,128)S(1)} %fusion.65), channel_id=1, replica_groups=mesh['rowa'=2,'rowb'=4,'col'=4] {'col'}, dimensions={1}, use_global_device_ids=true | all-gather | bytes 655360 | tf_op jit(solution)/shard_map/all_gather | solution.py:58
  261.3 1.5 cholesky.211
  264.1 1.2 custom-call.21
  265.6 0.7 gather_fusion
  267.4 0.8 copy.32
  (66 shorter events, 16.0 us)
Async XLA Ops:
  7.2 202.2 %all-reduce.2.cloned.1.call-start = ((), (), s32[]{:S(2)}) async-start(), calls=%async_computation.1 | async-start | bytes 2097152 | tf_op jit(solution)/shard_map/psum | solution.py:50
  67.1 10.4 %copy-start.1 = (f32[16,128]{1,0:T(8,128)S(1)}, f32[16,128]{1,0:T(8,128)}, u32[]{:S(2)}) copy-start(f32[16,128]{1,0:T(8,128)} %param.6) | copy-start | bytes 24580
  209.4 19.2 %copy-start = (f32[512,512]{1,0:T(8,128)S(1)}, f32[512,512]{1,0:T(8,128)}, u32[]{:S(2)}) copy-start(f32[512,512]{1,0:T(8,128)} %all-reduce.2.cloned.1.call-done) | copy-start | bytes 3145732
Sparse Core Ops, SparseCore 0:
  77.6 131.7 all-reduce.1
where the time goes:
time: 276 us; the launch traced here: 275 us
  waiting for transfers between devices  127 us (46%)
  blocking collectives  67 us (24%)
  other arithmetic  32.8 us (12%)
  matrix products  26.4 us (10%)
  between operations  14.2 us (5%)
  local copies, waits for them, and re-layouts  8.11 us (3%)
    psum x1, waiting for transfers between devices, on_device(): cover = lax.psum(partial_cover, ('rowa', 'rowb', 'col'))  126 us
    all_to_all x1, blocking collectives, on_device(): lax.all_to_all(table, 'col', split_axis=0, concat_axis=1, tiled=True)  54.6 us
    another operation x24, other arithmetic, normalize(): lower = jnp.linalg.cholesky(gram)  17.2 us
    another operation x16, other arithmetic, normalize(): jax.scipy.linalg.solve_triangular(lower, products, lower=True)  15 us
    dot_general x1, matrix products, on_device(): lax.dot_general(regrouped, regrouped, (((0,), (0,)), ((), ())), precision...  10.3 us
    dot_general x8, matrix products, on_device(): jnp.dot(vectors, cover, precision=high, preferred_element_type=jnp.float32)  8.81 us
    all_gather x1, blocking collectives, on_device(): left = lax.all_gather(images, 'col', axis=1, tiled=True)  7.1 us
  transfers between devices with their start and end apart: 1, of which 1 were waited for; matrix products, arithmetic and copies ran while one was open for 0% of the time, Pallas kernels for 0%

commit v1 on v0

v1 whole, which is shorter than its diff:
```python
import functools

import jax
import jax.numpy as jnp
from jax import lax
from jax.experimental import pallas as pl
from jax.experimental.pallas import tpu as pltpu
from jax.sharding import PartitionSpec as P

STEPS = 8
CHUNKS = 8
LEFT_CHUNKS = 4
CORES = 2
MESH = pl.DeviceIdType.MESH
high = lax.Precision.HIGHEST


def dot(a, b, dims):
    return lax.dot_general(a, b, (dims, ((), ())), precision=high, preferred_element_type=jnp.float32)


def orthonormal(products):
    block, cols = products.shape
    tiles = cols // 128
    gram = dot(products, products, ((1,), (1,)))
    column = [jnp.broadcast_to(gram[:, k : k + 1], (block, 128)) for k in range(block)]
    part = [products[:, t * 128 : (t + 1) * 128] for t in range(tiles)]
    row = lax.broadcasted_iota(jnp.int32, (block, 128), 0)
    lane = lax.broadcasted_iota(jnp.int32, (1, 128), 1)
    diagonal = jnp.zeros((1, 128), jnp.float32)
    for j in range(block):
        pivot = column[j][j : j + 1, :]
        inverse = lax.rsqrt(pivot)
        inverse = inverse * (1.5 - 0.5 * (pivot * inverse) * inverse)
        diagonal = jnp.where(lane == j, pivot * inverse, diagonal)
        below = jnp.where(row > j, column[j] * inverse, 0.0)
        for t in range(tiles):
            solved = part[t][j : j + 1, :] * inverse
            part[t] = jnp.where(row == j, solved, part[t] - below * solved)
        for k in range(j + 1, block):
            column[k] = column[k] - below * below[k : k + 1, :]
    return jnp.concatenate(part, axis=1), diagonal


def kernel(na, nb, nc, n_copies, table, start, right_ref, left_ref, strength_ref, *scratch):
    (blocks, extra, vecs, acc_d, acc_c, diag, cross, cover,
     d_core, d_a, d_b, c_core, c_hi, c_a, c_b, send, recv, local) = scratch
    nh = nc // CORES
    rows_dev, width = table.shape
    quarter = rows_dev // nc
    chunk = quarter // CHUNKS
    half = CORES * width
    a, b, col = lax.axis_index("rowa"), lax.axis_index("rowb"), lax.axis_index("col")
    core, hi = lax.rem(col, CORES), lax.div(col, CORES)
    at_a = lambda i: {"rowa": i}
    at_b = lambda i: {"rowb": i}
    at_col = lambda i: {"col": i}
    at_core = lambda i: {"col": hi * CORES + i}
    at_hi = lambda i: {"col": i * CORES + core}
    used = [0]

    barrier = pltpu.get_barrier_semaphore()
    others = ([at_a(lax.rem(a + d, na)) for d in range(1, na)] + [at_b(lax.rem(b + d, nb)) for d in range(1, nb)]
              + [at_col(lax.rem(col + d, nc)) for d in range(1, nc)])
    for other in others:
        pl.semaphore_signal(barrier, inc=1, device_id=other, device_id_type=MESH)
    pl.semaphore_wait(barrier, len(others))

    def remote(src, dst, where):
        i = used[0]
        used[0] += 1
        copy = pltpu.make_async_remote_copy(src_ref=src, dst_ref=dst, send_sem=send.at[i], recv_sem=recv.at[i],
                                            device_id=where, device_id_type=MESH)
        copy.start()
        return copy

    def aligned(x, n):
        return pl.multiple_of(x, n)

    copies = [pltpu.make_async_copy(table.at[pl.ds(aligned(col * quarter, 8), quarter)], blocks.at[col], local.at[0])]
    for h in range(1, nh):
        q = lax.rem(hi + h, nh) * CORES + core
        copies.append(pltpu.make_async_copy(table.at[pl.ds(aligned(q * quarter, 8), quarter)], extra.at[h - 1, core], local.at[h]))
    for c in copies:
        c.start()
    near = []
    peer = 1 - core
    q = hi * CORES + peer
    near.append(remote(table.at[pl.ds(aligned(q * quarter, 8), quarter)], blocks.at[col], at_core(peer)))
    for h in range(1, nh):
        q = lax.rem(hi + h, nh) * CORES + peer
        near.append(remote(table.at[pl.ds(aligned(q * quarter, 8), quarter)], extra.at[h - 1, core], at_core(peer)))
    vecs[col] = start[...]
    for d in range(1, nc):
        near.append(remote(start, vecs.at[col], at_col(lax.rem(col + d, nc))))
    far = []
    for k in range(CHUNKS):
        far.append([])
        for h in range(1, nh):
            for c in range(CORES):
                q = lax.rem(hi + h, nh) * CORES + lax.rem(core + c, CORES)
                far[k].append(remote(table.at[pl.ds(aligned(q * quarter + k * chunk, 8), chunk)],
                                     blocks.at[col, pl.ds(k * chunk, chunk)], at_col(q)))

    def allreduce(acc, out, stages, slots, over_b, gather):
        off, length = 0, half
        trail = []
        for (n, me, at), slot in zip(stages, slots):
            piece = length // n
            moved = []
            for d in range(1, n):
                to = lax.rem(me + d, n)
                moved.append(remote(acc.at[pl.ds(aligned(off + to * piece, 8), piece)], slot.at[d - 1], at(to)))
            yield
            for m in moved:
                m.wait()
            trail.append((off, length))
            off, length = off + me * piece, piece
            mine = pl.ds(aligned(off, 8), length)
            total = acc[mine]
            for d in range(1, n):
                total = total + slot[d - 1]
            acc[mine] = total
        mine = pl.ds(aligned(off, 8), length)
        over_b[b] = acc[mine]
        moved = [remote(over_b.at[b], over_b.at[b], at_b(lax.rem(b + d, nb))) for d in range(1, nb)]
        yield
        for m in moved:
            m.wait()
        total = over_b[0]
        for i in range(1, nb):
            total = total + over_b[i]
        out[mine] = total
        for (n, me, at), (above, longer) in list(zip(stages, trail))[::-1][:gather]:
            mine = pl.ds(aligned(off, 8), length)
            moved = [remote(out.at[mine], out.at[mine], at(lax.rem(me + d, n))) for d in range(1, n)]
            yield
            for m in moved:
                m.wait()
            off, length = above, longer

    def diagonal_parts():
        acc_d[...] = jnp.zeros_like(acc_d)
        for c in copies:
            c.wait()
        for n in near:
            n.wait()

        @pl.loop(0, CHUNKS)
        def _(k):
            rows = pl.ds(aligned(k * chunk, 8), chunk)
            own = jnp.concatenate([blocks[hi * CORES + i, rows] for i in range(CORES)], axis=1)
            total = acc_d[...] + dot(own, own, ((0,), (0,)))
            for h in range(1, nh):
                own = jnp.concatenate([extra[h - 1, i, rows] for i in range(CORES)], axis=1)
                total = total + dot(own, own, ((0,), (0,)))
            acc_d[...] = total

        mine = diag.at[hi]
        yield from allreduce(acc_d, mine, [(CORES, core, at_core), (na, a, at_a)], [d_core, d_a], d_b, 1)
        rows = pl.ds(aligned(core * (half // CORES), 8), half // CORES)
        moved = [remote(mine.at[rows], mine.at[rows], at_hi(lax.rem(hi + h, nh))) for h in range(1, nh)]
        yield
        for m in moved:
            m.wait()
        moved = [remote(diag.at[:, rows], diag.at[:, rows], at_core(peer))]
        yield
        for m in moved:
            m.wait()

    def cross_chunk(k):
        for m in far[k]:
            m.wait()
        rows = pl.ds(k * chunk, chunk)
        left = jnp.concatenate([blocks[i, rows] for i in range(CORES)], axis=1)
        rest = jnp.concatenate([blocks[i, rows] for i in range(CORES, nc)], axis=1)
        new = dot(left, rest, ((0,), (0,)))
        acc_c[...] = new if k == 0 else acc_c[...] + new

    beside = diagonal_parts()
    next(beside)
    for k in range(CHUNKS):
        cross_chunk(k)
        if k < CHUNKS - 1 and k < 4:
            next(beside)
    stages = [(CORES, core, at_core), (nh, hi, at_hi), (na, a, at_a)]
    for i, _ in enumerate(allreduce(acc_c, cross, stages, [c_core, c_hi, c_a], c_b, 3)):
        if i == 4:
            next(beside)
    for _ in beside:
        pass
    for h in range(nh):
        cover[h * half : (h + 1) * half, h * half : (h + 1) * half] = diag[h]
    cover[:half, half:] = cross[...]
    cover[half:, :half] = cross[...].T

    vectors = jnp.concatenate([vecs[i] for i in range(nc)], axis=1)

    def step(_, vectors):
        return orthonormal(dot(vectors, cover[...], ((1,), (0,))))[0]

    previous = lax.fori_loop(0, STEPS - 1, step, vectors)
    moved, sent = [], []
    rows = quarter // LEFT_CHUNKS
    for k in range(LEFT_CHUNKS):
        piece = jnp.concatenate([blocks[i, pl.ds(k * rows, rows)] for i in range(nc)], axis=1)
        place = pl.ds(aligned(col * quarter + k * rows, 128), rows)
        left_ref[:, place] = dot(previous, piece, ((1,), (1,)))
        moved.append([remote(left_ref.at[:, place], left_ref.at[:, place], at_hi(lax.rem(hi + h, nh))) for h in range(1, nh)])
        sent.append(remote(left_ref.at[:, place], left_ref.at[:, place], at_core(peer)))
    vectors, diagonal = orthonormal(dot(previous, cover[...], ((1,), (0,))))
    for i in range(nc):
        vecs[i] = vectors[:, i * width : (i + 1) * width]
    right_ref[...] = vecs[col]
    strength_ref[...] = diagonal[:, : strength_ref.shape[1]] / (rows_dev * na * nb)
    for k in range(LEFT_CHUNKS):
        for h, m in enumerate(moved[k]):
            m.wait()
            q = lax.rem(hi + nh - (h + 1), nh) * CORES + core
            place = pl.ds(aligned(q * quarter + k * rows, 128), rows)
            sent.append(remote(left_ref.at[:, place], left_ref.at[:, place], at_core(peer)))
    for s in sent:
        s.wait()
    assert used[0] <= n_copies, used


def solution(mesh):
    na, nb, nc = mesh.shape["rowa"], mesh.shape["rowb"], mesh.shape["col"]
    nh = nc // CORES

    def on_device(table, start):
        rows_dev, width = table.shape
        block = start.shape[0]
        quarter, half = rows_dev // nc, CORES * width
        f32 = jnp.float32
        n_copies = 256
        vmem = pltpu.VMEM
        quad = half // CORES
        right, left, strength = pl.pallas_call(
            functools.partial(kernel, na, nb, nc, n_copies),
            out_shape=(
                jax.ShapeDtypeStruct((block, width), f32),
                jax.ShapeDtypeStruct((block, rows_dev), f32),
                jax.ShapeDtypeStruct((1, block), f32),
            ),
            in_specs=[pl.BlockSpec(memory_space=pl.ANY), pl.BlockSpec(memory_space=pltpu.VMEM)],
            out_specs=tuple([pl.BlockSpec(memory_space=pltpu.VMEM)] * 3),
            scratch_shapes=[
                vmem((nc, quarter, width), f32),
                vmem((nh - 1, CORES, quarter, width), f32),
                vmem((nc, block, width), f32),
                vmem((half, half), f32),
                vmem((half, half), f32),
                vmem((nh, half, half), f32),
                vmem((half, half), f32),
                vmem((nc * width, nc * width), f32),
                vmem((CORES - 1, quad, half), f32),
                vmem((na - 1, quad // na, half), f32),
                vmem((nb, quad // na, half), f32),
                vmem((CORES - 1, quad, half), f32),
                vmem((nh - 1, quad // nh, half), f32),
                vmem((na - 1, quad // nh // na, half), f32),
                vmem((nb, quad // nh // na, half), f32),
                pltpu.SemaphoreType.DMA((n_copies,)),
                pltpu.SemaphoreType.DMA((n_copies,)),
                pltpu.SemaphoreType.DMA((nh,)),
            ],
            compiler_params=pltpu.CompilerParams(
                collective_id=0, has_side_effects=True, vmem_limit_bytes=48 * 1024 * 1024
            ),
        )(table, start)
        return right, left, strength.reshape(block)

    return jax.shard_map(
        on_device,
        mesh=mesh,
        in_specs=(P(("rowa", "rowb"), "col"), P(None, "col")),
        out_specs=(P(None, "col"), P(None, ("rowa", "rowb")), P()),
        check_vma=False,
    )
```

time: 276 us -> 97 us (0.35)
  waiting for transfers between devices: 127 us -> 0 us
  Pallas kernels: 0 us -> 91.3 us
  blocking collectives: 67 us -> 0 us
  other arithmetic: 32.8 us -> 0 us
  matrix products: 26.4 us -> 0 us
  between operations: 14.2 us -> 0.65 us
  local copies, waits for them, and re-layouts: 8.11 us -> 4.78 us
    psum x1 -> x0, waiting for transfers between devices: 126 us -> none  [on_device(): cover = lax.psum(partial_cover, ('rowa', 'rowb', 'col'))]
    pallas_call x0 -> x1, Pallas kernels: none -> 91.3 us  [on_device(): pl.pallas_call(functools.partial(kernel, na, nb, nc, n_copies), out_shape...]
    all_to_all x1 -> x0, blocking collectives: 54.6 us -> none  [on_device(): lax.all_to_all(table, 'col', split_axis=0, concat_axis=1, tiled=True)]
    another operation x40 -> x0, other arithmetic: 32.2 us -> none  [the longest x24 17.2 us: normalize(): lower = jnp.linalg.cholesky(gram)]
    dot_general x18 -> x0, matrix products: 24.6 us -> none  [the longest x1 10.3 us: on_device(): lax.dot_general(regrouped, regrouped, (((0,), (0,)), ((), ())), precision...]
    all_gather x2 -> x0, blocking collectives: 12.5 us -> none  [the longest x1 7.1 us: on_device(): left = lax.all_gather(images, 'col', axis=1, tiled=True)]
    all_to_all x1 -> x0, local copies, waits for them, and re-layouts: 5.37 us -> none  [on_device(): lax.all_to_all(table, 'col', split_axis=0, concat_axis=1, tiled=True)]
    unnamed x5 -> x7, local copies, waits for them, and re-layouts: 0.82 us -> 4.78 us
  transfers between devices with their start and end apart: 1 -> 0, of which waited for: 1 -> 0; matrix products, arithmetic and copies ran while one was open for 0% -> 0% of each run, Pallas kernels for 0% -> 0%
where the time goes in v1:
time: 97 us; the launch traced here: 96.8 us
  Pallas kernels  91.3 us (94%)
  local copies, waits for them, and re-layouts  4.78 us (5%)
    pallas_call x1, Pallas kernels, on_device(): pl.pallas_call(functools.partial(kernel, na, nb, nc, n_copies), out_shape...  91.3 us
    unnamed x7, local copies, waits for them, and re-layouts  4.78 us

profile of v1, /device:TPU:0, one launch (start us, length us, event | category | flops | bytes accessed | tf_op | source)
XLA Modules:
  0.0 96.8 jit_solution(2135222154659083247)
XLA Ops:
  0.6 0.0 copy-start
  0.6 2.2 %copy-done = f32[8192,128]{1,0:T(8,128)S(1)} copy-done((f32[8192,128]{1,0:T(8,128)S(1)}, f32[8192,128]{1,0:T(8,128)}, u32[]{:S(2)}) %copy-start) | copy-done | bytes 4194328
  2.8 0.0 copy-start.1
  2.8 0.7 copy-done.1
  3.5 91.3 %shard_map.49 = (f32[16,128]{1,0:T(8,128)S(1)}, f32[16,8192]{1,0:T(8,128)S(1)}, f32[1,16]{1,0:T(1,128)S(1)}) custom-call(f32[8192,128]{1,0:T(8,128)S(1)} %copy-done, f32[16,128]{1,0:T(8,128)S(1)} %copy-done.1), custom_call_target="tpu_custom_call" | custom-call | tf_op jit(solution)/shard_map/pallas_call | solution.py:239
  94.9 0.6 copy.8
  95.5 0.8 copy.9
  96.3 0.5 copy.10
Async XLA Ops:
  0.6 2.2 %copy-start = (f32[8192,128]{1,0:T(8,128)S(1)}, f32[8192,128]{1,0:T(8,128)}, u32[]{:S(2)}) copy-start(f32[8192,128]{1,0:T(8,128)} %table.1) | copy-start | bytes 12582916
  2.8 0.7 copy-start.1

commit v2 on v1

--- a/solution.py
+++ b/solution.py
@@ -44,7 +44,7 @@
 
 def kernel(na, nb, nc, n_copies, table, start, right_ref, left_ref, strength_ref, *scratch):
     (blocks, extra, vecs, acc_d, acc_c, diag, cross, cover,
-     d_core, d_a, d_b, c_core, c_hi, c_a, c_b, send, recv, local) = scratch
+     d_core, d_a, d_b, c_core, c_group, c_b, held, coarse, fine, send, recv, local) = scratch
     nh = nc // CORES
     rows_dev, width = table.shape
     quarter = rows_dev // nc
@@ -57,14 +57,11 @@
     at_col = lambda i: {"col": i}
     at_core = lambda i: {"col": hi * CORES + i}
     at_hi = lambda i: {"col": i * CORES + core}
+    at_group = lambda i: {"rowa": lax.rem(i, na), "col": lax.div(i, na) * CORES + core}
     used = [0]
 
-    barrier = pltpu.get_barrier_semaphore()
-    others = ([at_a(lax.rem(a + d, na)) for d in range(1, na)] + [at_b(lax.rem(b + d, nb)) for d in range(1, nb)]
-              + [at_col(lax.rem(col + d, nc)) for d in range(1, nc)])
-    for other in others:
-        pl.semaphore_signal(barrier, inc=1, device_id=other, device_id_type=MESH)
-    pl.semaphore_wait(barrier, len(others))
+    def aligned(x, n):
+        return pl.multiple_of(x, n)
 
     def remote(src, dst, where):
         i = used[0]
@@ -74,33 +71,51 @@
         copy.start()
         return copy
 
-    def aligned(x, n):
-        return pl.multiple_of(x, n)
-
-    copies = [pltpu.make_async_copy(table.at[pl.ds(aligned(col * quarter, 8), quarter)], blocks.at[col], local.at[0])]
+    peer = 1 - core
+    order = [lax.rem(hi + h, nh) * CORES + lax.rem(core + c, CORES) for h in range(1, nh) for c in range(CORES)]
+    loads = []
+
+    def load(src, dst):
+        copy = pltpu.make_async_copy(src, dst, local.at[len(loads)])
+        copy.start()
+        loads.append(copy)
+
+    for q in order + [hi * CORES + peer]:
+        rows = pl.ds(aligned(q * quarter, 8), quarter)
+        load(table.at[rows], held.at[rows])
+    load(start, vecs.at[col])
+    load(table.at[pl.ds(aligned(col * quarter, 8), quarter)], blocks.at[col])
     for h in range(1, nh):
         q = lax.rem(hi + h, nh) * CORES + core
-        copies.append(pltpu.make_async_copy(table.at[pl.ds(aligned(q * quarter, 8), quarter)], extra.at[h - 1, core], local.at[h]))
-    for c in copies:
-        c.start()
+        load(table.at[pl.ds(aligned(q * quarter, 8), quarter)], extra.at[h - 1, core])
+    copies = loads[len(order) + 2 :]
+
+    barrier = pltpu.get_barrier_semaphore()
+    others = ([at_a(lax.rem(a + d, na)) for d in range(1, na)] + [at_b(lax.rem(b + d, nb)) for d in range(1, nb)]
+              + [at_col(lax.rem(col + d, nc)) for d in range(1, nc)]
+              + [at_group(lax.rem(hi + h, nh) * na + lax.rem(a + d, na)) for h in range(1, nh) for d in range(1, na)])
+    for other in others:
+        pl.semaphore_signal(barrier, inc=1, device_id=other, device_id_type=MESH)
+    pl.semaphore_wait(barrier, len(others))
+
+    for c in loads[: len(order) + 2]:
+        c.wait()
     near = []
-    peer = 1 - core
-    q = hi * CORES + peer
-    near.append(remote(table.at[pl.ds(aligned(q * quarter, 8), quarter)], blocks.at[col], at_core(peer)))
-    for h in range(1, nh):
-        q = lax.rem(hi + h, nh) * CORES + peer
-        near.append(remote(table.at[pl.ds(aligned(q * quarter, 8), quarter)], extra.at[h - 1, core], at_core(peer)))
-    vecs[col] = start[...]
     for d in range(1, nc):
-        near.append(remote(start, vecs.at[col], at_col(lax.rem(col + d, nc))))
+        near.append(remote(vecs.at[col], vecs.at[col], at_col(lax.rem(col + d, nc))))
     far = []
     for k in range(CHUNKS):
         far.append([])
         for h in range(1, nh):
             for c in range(CORES):
                 q = lax.rem(hi + h, nh) * CORES + lax.rem(core + c, CORES)
-                far[k].append(remote(table.at[pl.ds(aligned(q * quarter + k * chunk, 8), chunk)],
+                far[k].append(remote(held.at[pl.ds(aligned(q * quarter + k * chunk, 8), chunk)],
                                      blocks.at[col, pl.ds(k * chunk, chunk)], at_col(q)))
+    q = hi * CORES + peer
+    near.append(remote(held.at[pl.ds(aligned(q * quarter, 8), quarter)], blocks.at[col], at_core(peer)))
+    for h in range(1, nh):
+        q = lax.rem(hi + h, nh) * CORES + peer
+        near.append(remote(held.at[pl.ds(aligned(q * quarter, 8), quarter)], extra.at[h - 1, core], at_core(peer)))
 
     def allreduce(acc, out, stages, slots, over_b, gather):
         off, length = 0, half
@@ -172,9 +187,12 @@
         for m in far[k]:
             m.wait()
         rows = pl.ds(k * chunk, chunk)
-        left = jnp.concatenate([blocks[i, rows] for i in range(CORES)], axis=1)
-        rest = jnp.concatenate([blocks[i, rows] for i in range(CORES, nc)], axis=1)
-        new = dot(left, rest, ((0,), (0,)))
+        whole = jnp.concatenate([blocks[i, rows] for i in range(nc)], axis=1)
+        turned = whole.T
+        large = turned.astype(jnp.bfloat16)
+        coarse[:, rows] = large
+        fine[:, rows] = (turned - large.astype(jnp.float32)).astype(jnp.bfloat16)
+        new = dot(turned[:half], whole[:, half:], ((1,), (0,)))
         acc_c[...] = new if k == 0 else acc_c[...] + new
 
     beside = diagonal_parts()
@@ -183,9 +201,9 @@
         cross_chunk(k)
         if k < CHUNKS - 1 and k < 4:
             next(beside)
-    stages = [(CORES, core, at_core), (nh, hi, at_hi), (na, a, at_a)]
-    for i, _ in enumerate(allreduce(acc_c, cross, stages, [c_core, c_hi, c_a], c_b, 3)):
-        if i == 4:
+    stages = [(CORES, core, at_core), (nh * na, hi * na + a, at_group)]
+    for i, _ in enumerate(allreduce(acc_c, cross, stages, [c_core, c_group], c_b, 2)):
+        if i == 3:
             next(beside)
     for _ in beside:
         pass
@@ -202,10 +220,16 @@
     previous = lax.fori_loop(0, STEPS - 1, step, vectors)
     moved, sent = [], []
     rows = quarter // LEFT_CHUNKS
+    large = previous.astype(jnp.bfloat16)
+    small = (previous - large.astype(jnp.float32)).astype(jnp.bfloat16)
+    block = previous.shape[0]
+    both = jnp.concatenate([large, small], axis=0)
     for k in range(LEFT_CHUNKS):
-        piece = jnp.concatenate([blocks[i, pl.ds(k * rows, rows)] for i in range(nc)], axis=1)
+        piece = pl.ds(k * rows, rows)
+        main = jnp.dot(both, coarse[:, piece], preferred_element_type=jnp.float32)
+        rest = jnp.dot(large, fine[:, piece], preferred_element_type=jnp.float32)
         place = pl.ds(aligned(col * quarter + k * rows, 128), rows)
-        left_ref[:, place] = dot(previous, piece, ((1,), (1,)))
+        left_ref[:, place] = main[:block] + (main[block:] + rest)
         moved.append([remote(left_ref.at[:, place], left_ref.at[:, place], at_hi(lax.rem(hi + h, nh))) for h in range(1, nh)])
         sent.append(remote(left_ref.at[:, place], left_ref.at[:, place], at_core(peer)))
     vectors, diagonal = orthonormal(dot(previous, cover[...], ((1,), (0,))))
@@ -222,6 +246,15 @@
     for s in sent:
         s.wait()
     assert used[0] <= n_copies, used
+
+
+def hand_out(*refs):
+    sems = refs[-1]
+    copies = [pltpu.make_async_copy(refs[i], refs[3 + i], sems.at[i]) for i in range(3)]
+    for c in copies:
+        c.start()
+    for c in copies:
+        c.wait()
 
 
 def solution(mesh):
@@ -243,7 +276,7 @@
                 jax.ShapeDtypeStruct((block, rows_dev), f32),
                 jax.ShapeDtypeStruct((1, block), f32),
             ),
-            in_specs=[pl.BlockSpec(memory_space=pl.ANY), pl.BlockSpec(memory_space=pltpu.VMEM)],
+            in_specs=[pl.BlockSpec(memory_space=pl.ANY), pl.BlockSpec(memory_space=pl.ANY)],
             out_specs=tuple([pl.BlockSpec(memory_space=pltpu.VMEM)] * 3),
             scratch_shapes=[
                 vmem((nc, quarter, width), f32),
@@ -258,17 +291,26 @@
                 vmem((na - 1, quad // na, half), f32),
                 vmem((nb, quad // na, half), f32),
                 vmem((CORES - 1, quad, half), f32),
-                vmem((nh - 1, quad // nh, half), f32),
-                vmem((na - 1, quad // nh // na, half), f32),
+                vmem((nh * na - 1, quad // nh // na, half), f32),
                 vmem((nb, quad // nh // na, half), f32),
+                vmem((rows_dev, width), f32),
+                vmem((nc * width, quarter), jnp.bfloat16),
+                vmem((nc * width, quarter), jnp.bfloat16),
                 pltpu.SemaphoreType.DMA((n_copies,)),
                 pltpu.SemaphoreType.DMA((n_copies,)),
-                pltpu.SemaphoreType.DMA((nh,)),
+                pltpu.SemaphoreType.DMA((nc + nh + 1,)),
             ],
             compiler_params=pltpu.CompilerParams(
-                collective_id=0, has_side_effects=True, vmem_limit_bytes=48 * 1024 * 1024
+                collective_id=0, has_side_effects=True, vmem_limit_bytes=60 * 1024 * 1024
             ),
         )(table, start)
+        right, left, strength = pl.pallas_call(
+            hand_out,
+            out_shape=tuple(jax.ShapeDtypeStruct(x.shape, f32) for x in (right, left, strength)),
+            in_specs=[pl.BlockSpec(memory_space=pltpu.VMEM)] * 3,
+            out_specs=tuple([pl.BlockSpec(memory_space=pl.ANY)] * 3),
+            scratch_shapes=[pltpu.SemaphoreType.DMA((3,))],
+        )(right, left, strength)
         return right, left, strength.reshape(block)
 
     return jax.shard_map(

time: 97 us -> 89.1 us (0.919)
  local copies, waits for them, and re-layouts: 4.78 us -> 0 us
  Pallas kernels: 91.3 us -> 88.3 us
    pallas_call x1, Pallas kernels: 91.3 us -> 86.5 us  [on_device(): pl.pallas_call(functools.partial(kernel, na, nb, nc, n_copies), out_shape...]
    unnamed x7 -> x0, local copies, waits for them, and re-layouts: 4.78 us -> none
    pallas_call x0 -> x1, Pallas kernels: none -> 1.87 us  [on_device(): pl.pallas_call(hand_out, out_shape=tuple((jax.ShapeDtypeStruct(x.shape, f...]
where the time goes in v2:
time: 89.1 us; the launch traced here: 89 us
  Pallas kernels  88.3 us (99%)
    pallas_call x1, Pallas kernels, on_device(): pl.pallas_call(functools.partial(kernel, na, nb, nc, n_copies), out_shape...  86.5 us
    pallas_call x1, Pallas kernels, on_device(): pl.pallas_call(hand_out, out_shape=tuple((jax.ShapeDtypeStruct(x.shape, f...  1.87 us

profile of v2, /device:TPU:0, one launch (start us, length us, event | category | flops | bytes accessed | tf_op | source)
XLA Modules:
  0.0 89.0 jit_solution(4516683167834210675)
XLA Ops:
  0.6 86.5 %shard_map.49 = (f32[16,128]{1,0:T(8,128)}, f32[16,8192]{1,0:T(8,128)}, f32[1,16]{1,0:T(1,128)}) custom-call(f32[8192,128]{1,0:T(8,128)} %table.1, f32[16,128]{1,0:T(8,128)} %start.1), custom_call_target="tpu_custom_call" | custom-call | tf_op jit(solution)/shard_map/pallas_call | solution.py:272
  87.1 1.9 %shard_map.50 = (f32[16,128]{1,0:T(8,128)}, f32[16,8192]{1,0:T(8,128)}, f32[1,16]{1,0:T(1,128)}) custom-call(f32[16,128]{1,0:T(8,128)} %get-tuple-element.9.refs_0_, f32[16,8192]{1,0:T(8,128)} %get-tuple-element.10.refs_1_, f32[1,16]{1,0:T(1,128)} %get-tuple-element.11.refs_2_), custom_call_target="tpu_custom_call" | custom-call | tf_op jit(solution)/shard_map/pallas_call | solution.py:307

commit v3 on v2

--- a/solution.py
+++ b/solution.py
@@ -8,7 +8,7 @@
 from jax.sharding import PartitionSpec as P
 
 STEPS = 8
-CHUNKS = 8
+CHUNKS = 16
 LEFT_CHUNKS = 4
 CORES = 2
 MESH = pl.DeviceIdType.MESH

time: 89.1 us -> 89.1 us (level)
  no operation moved by 1% of the time
where the time goes in v3:
time: 89.1 us; the launch traced here: 88.9 us
  Pallas kernels  88.3 us (99%)
    pallas_call x1, Pallas kernels, on_device(): pl.pallas_call(functools.partial(kernel, na, nb, nc, n_copies), out_shape...  86.4 us
    pallas_call x1, Pallas kernels, on_device(): pl.pallas_call(hand_out, out_shape=tuple((jax.ShapeDtypeStruct(x.shape, f...  1.87 us

profile of v3, /device:TPU:0, one launch (start us, length us, event | category | flops | bytes accessed | tf_op | source)
XLA Modules:
  0.0 88.9 jit_solution(1908489246306404444)
XLA Ops:
  0.6 86.4 %shard_map.49 = (f32[16,128]{1,0:T(8,128)}, f32[16,8192]{1,0:T(8,128)}, f32[1,16]{1,0:T(1,128)}) custom-call(f32[8192,128]{1,0:T(8,128)} %table.1, f32[16,128]{1,0:T(8,128)} %start.1), custom_call_target="tpu_custom_call" | custom-call | tf_op jit(solution)/shard_map/pallas_call | solution.py:272
  87.1 1.9 %shard_map.50 = (f32[16,128]{1,0:T(8,128)}, f32[16,8192]{1,0:T(8,128)}, f32[1,16]{1,0:T(1,128)}) custom-call(f32[16,128]{1,0:T(8,128)} %get-tuple-element.9.refs_0_, f32[16,8192]{1,0:T(8,128)} %get-tuple-element.10.refs_1_, f32[1,16]{1,0:T(1,128)} %get-tuple-element.11.refs_2_), custom_call_target="tpu_custom_call" | custom-call | tf_op jit(solution)/shard_map/pallas_call | solution.py:307
